TPU v7x, 8 devices: a whole 2x2x1 slice. The times are simulated.
8 devices in a mesh: data: 2 (over z, y), model: 4 (over x, core).
Axes of the slice: x: 2, y: 2, z: 1, core: 2. Of those that a mesh axis runs over, the one named last changes fastest.
Arguments:
- hidden: bfloat16 [8192, 5120], P('data', 'model')
- unembed: bfloat16 [32000, 5120], P('model', 'data')
- draft_ids: int32 [8192], P('data')
- q_prob: float32 [8192], P('data')
Outputs:
- output 1: float32 [8192], P('data')
- output 2: float32 [8192], P('data')
All inputs are finite; a program needn't handle non-finite values.
Results may differ from a plain program's by a relative error of at most 0.001.
Values are sent between devices in bfloat16 or wider.
A program may use at most 1 GiB of HBM per device.

v0:
```python
import jax
import jax.numpy as jnp
from jax import lax
from jax.sharding import PartitionSpec as P


def solution(mesh):
    def per_device(h_part, w_part, draft_loc, q_loc):
        h_rows = lax.all_gather(h_part, "model", axis=1, tiled=True)
        w_rows = lax.all_gather(w_part, "data", axis=1, tiled=True)
        logits = lax.dot_general(h_rows, w_rows, (((1,), (1,)), ((), ())), preferred_element_type=jnp.float32)
        shard_vocab = w_rows.shape[0]
        row_max = lax.pmax(jnp.max(logits, axis=1), "model")
        local_sum = jnp.sum(jnp.exp(logits - row_max[:, None]), axis=1)
        vocab_ids = lax.axis_index("model") * shard_vocab + lax.broadcasted_iota(jnp.int32, (1, shard_vocab), 1)
        local_pick = jnp.sum(jnp.where(vocab_ids == draft_loc[:, None], logits, 0.0), axis=1)
        totals = lax.psum(jnp.stack([local_sum, local_pick]), "model")
        log_prob = totals[1] - row_max - jnp.log(totals[0])
        accept = jnp.minimum(1.0, jnp.exp(log_prob) / q_loc)
        return log_prob, accept

    return jax.shard_map(per_device, mesh=mesh, in_specs=(P("data", "model"), P("model", "data"), P("data"), P("data")), out_specs=(P("data"), P("data")), check_vma=False)
```

profile of v0, /device:TPU:0, one launch (start us, length us, event | category | flops | bytes accessed | tf_op | source)
XLA Modules:
  0.0 1617.2 jit_solution(14990456755878078814)
XLA Ops:
  7.2 0.0 all-gather.3.cloned.1.call-start
  7.2 0.7 all-gather.3.cloned.1.call-update
  7.9 0.0 all-gather.5.cloned.1.call-start
  7.9 0.7 all-gather.5.cloned.1.call-update
  8.7 0.6 iota_add_fusion
  9.3 251.1 %all-gather.3.cloned.1.call-done = bf16[4096,5120]{1,0:T(8,128)(2,1)} async-done(((bf16[4096,1280]{1,0:T(8,128)(2,1)}), bf16[4096,5120]{1,0:T(8,128)(2,1)}) %all-gather.3.cloned.1.call-update) | async-done | bytes 41943056 | tf_op jit(solution)/shard_map/all_gather | solution.py:9
  260.4 931.8 %all-gather.5.cloned.1.call-done = bf16[8000,5120]{1,0:T(8,128)(2,1)} async-done(((bf16[8000,2560]{1,0:T(8,128)(2,1)}), bf16[8000,5120]{1,0:T(8,128)(2,1)}) %all-gather.5.cloned.1.call-update) | async-done | bytes 81920016 | tf_op jit(solution)/shard_map/all_gather | solution.py:10
  1192.1 0.0 copy-start
  1192.1 0.0 copy-start.1
  1192.1 356.0 %fusion.1 = (f32[4096]{0:T(1024)S(1)}, f32[4096,8000]{0,1:T(8,128)}) fusion(bf16[4096,5120]{1,0:T(8,128)(2,1)} %all-gather.3.cloned.1.call-done, bf16[8000,5120]{1,0:T(8,128)(2,1)} %all-gather.5.cloned.1.call-done), kind=kOutput, calls=%fused_computation.8 | convolution fusion | flops 335577088000 | bytes 254951424 | tf_op jit(solution)/shard_map/dot_general | solution.py:11
  1548.1 0.0 copy-start.2
  1548.1 10.7 pmax.7
  1558.9 0.0 copy-done
  1558.9 0.0 copy-done.1
  1558.9 40.5 %exponential_reduce_fusion = (f32[4096]{0:T(1024)S(1)}, f32[4096]{0:T(1024)S(1)}) fusion(f32[4096,8000]{0,1:T(8,128)} %get-tuple-element.9, f32[4096]{0:T(1024)S(1)} %pmax.7, s32[4096]{0:T(1024)S(1)} %copy-done.1, s32[8000]{0:T(1024)S(1)} %copy-done), kind=kLoop, calls=%fused_computation.1 | loop fusion | flops 163831808 | bytes 131169536 | tf_op jit(solution)/shard_map/reduce_sum | solution.py:14
  1599.4 10.3 psum.7
  1609.7 0.0 copy-done.2
  1609.7 0.6 divide_minimum_fusion
  (2 shorter events, 0.1 us)
Async XLA Ops:
  7.2 253.2 %all-gather.3.cloned.1.call-start = ((), (), s32[]{:S(2)}) async-start(), calls=%async_computation | async-start | bytes 52428800 | tf_op jit(solution)/shard_map/all_gather | solution.py:9
  7.9 1184.2 %all-gather.5.cloned.1.call-start = ((), (), s32[]{:S(2)}) async-start(), calls=%async_computation.1 | async-start | bytes 122880000 | tf_op jit(solution)/shard_map/all_gather | solution.py:10
  1192.1 366.7 %copy-start = (s32[8000]{0:T(1024)S(1)}, s32[8000]{0:T(1024)}, u32[]{:S(2)}) copy-start(s32[8000]{0:T(1024)} %iota_add_fusion) | copy-start | bytes 96004
  1192.1 366.7 %copy-start.1 = (s32[4096]{0:T(1024)S(1)}, s32[4096]{0:T(1024)}, u32[]{:S(2)}) copy-start(s32[4096]{0:T(1024)} %param.6) | copy-start | bytes 49156
  1548.1 61.6 %copy-start.2 = (f32[4096]{0:T(1024)S(1)}, f32[4096]{0:T(1024)}, u32[]{:S(2)}) copy-start(f32[4096]{0:T(1024)} %param.7) | copy-start | bytes 49156
Sparse Core Ops, SparseCore 0:
  9.5 250.8 all-gather.2
  261.9 930.1 all-gather.4
where the time goes:
time: 1620 us
  waiting for transfers between devices  1180 us (73%)
  matrix products  356 us (22%)
  other arithmetic  41.7 us (3%)
  blocking collectives  21 us (1%)
    all_gather x1, waiting for transfers between devices, per_device(): w_rows = lax.all_gather(w_part, 'data', axis=1, tiled=True)  932 us
    dot_general x1, matrix products, per_device(): lax.dot_general(h_rows, w_rows, (((1,), (1,)), ((), ())), preferred_eleme...  356 us
    all_gather x1, waiting for transfers between devices, per_device(): h_rows = lax.all_gather(h_part, 'model', axis=1, tiled=True)  251 us
    reduce_sum x1, other arithmetic, per_device(): local_sum = jnp.sum(jnp.exp(logits - row_max[:, None]), axis=1)  40.5 us
  transfers between devices with their start and end apart: 2, of which 2 were waited for; matrix products, arithmetic and copies ran while one was open for 0% of the time, Pallas kernels for 0%

commit v1 on v0

v1 whole, which is shorter than its diff:
```python
import functools

import jax
import jax.numpy as jnp
from jax import lax
from jax.experimental import pallas as pl
from jax.experimental.pallas import tpu as pltpu
from jax.sharding import PartitionSpec as P

MESH = pl.DeviceIdType.MESH
WC = 400
R1 = 512
PIECE = 128
R2 = 256


def _kernel(rows, quarter, shard, half, h_ref, w_ref, d_ref, q_ref, lp_ref, ac_ref, ha_ref,
            wv, hb, dv, st1, sta, stb, own_sem, ld_sem, d_sem, w_ss, w_rs, y_ss, y_rs,
            x1_ss, x1_rs, d1_ss, d1_rs, f1_ss, f1_rs, x2_ss, x2_rs, d2_ss, d2_rs, f2_ss, f2_rs,
            sa_ss, sa_rs, sb_ss, sb_rs):
    y = lax.axis_index("data")
    m = lax.axis_index("model")
    x = m // 2
    c = m % 2
    oy = 1 - y
    ox = 1 - x
    oc = 1 - c
    me_id = (y, m)
    dev_y = (oy, m)
    dev_x = (y, ox * 2 + c)
    dev_d = (y, x * 2 + oc)
    vocab = shard // 2
    base = m * shard + y * vocab
    n_wc = vocab // WC
    n_rb = rows // R1
    n_pc = rows // PIECE
    n_b2 = rows // R2

    def col(p):
        return pl.ds(pl.multiple_of(p * quarter, 128), quarter)

    def whalf(hh):
        return pl.ds(pl.multiple_of(lax.rem(hh + x, 2) * half, 128), half)

    def peer(k):
        kx, kc = k // 2, k % 2
        return lax.rem(x + kx, 2) * 2 + lax.rem(c + kc, 2)

    bar = pltpu.get_barrier_semaphore()
    for dy in range(2):
        for k in range(4):
            if dy or k:
                pl.semaphore_signal(bar, 1, device_id=(lax.rem(y + dy, 2), peer(k)), device_id_type=MESH)
    pl.semaphore_wait(bar, 7)

    def rcopy(src, dst, ss, rs, dev):
        return pltpu.make_async_remote_copy(src, dst, ss, rs, device_id=dev, device_id_type=MESH)

    def w_copy(j):
        return rcopy(w_ref.at[pl.ds(pl.multiple_of(oy * vocab + j * WC, 16), WC)],
                     wv.at[pl.ds(pl.multiple_of(j * WC, 16), WC), whalf(y)], w_ss.at[j], w_rs.at[j], dev_y)

    def w_wait(j):
        rcopy(w_ref.at[pl.ds(0, WC)], wv.at[pl.ds(pl.multiple_of(j * WC, 16), WC), whalf(oy)],
              w_ss.at[j], w_rs.at[j], dev_y).wait_recv()

    def prow(yy, t):
        return pl.ds(pl.multiple_of(yy * rows + t * PIECE, PIECE), PIECE)

    def y_copy(t):
        return rcopy(h_ref.at[pl.ds(pl.multiple_of(t * PIECE, PIECE), PIECE)], ha_ref.at[prow(y, t), col(c)],
                     y_ss.at[t], y_rs.at[t], dev_y)

    def y_wait(t):
        rcopy(h_ref.at[pl.ds(0, PIECE)], ha_ref.at[prow(oy, t), col(c)], y_ss.at[t], y_rs.at[t], dev_y).wait_recv()

    def rrow(i):
        return pl.ds(pl.multiple_of(y * rows + i * R1, R1), R1)

    def x1_copy(i):
        return rcopy(h_ref.at[pl.ds(pl.multiple_of(i * R1, R1), R1)], ha_ref.at[rrow(i), col(2 + c)],
                     x1_ss.at[i], x1_rs.at[i], dev_x)

    def d1_copy(pos):
        return rcopy(h_ref, ha_ref.at[pl.ds(pl.multiple_of(y * rows, R1), rows), col(pos)],
                     d1_ss, d1_rs, dev_d)

    def f1_copy(i, pos):
        return rcopy(ha_ref.at[rrow(i), col(2 + c)], ha_ref.at[rrow(i), col(2 + pos)],
                     f1_ss.at[i], f1_rs.at[i], dev_d)

    def x2_copy(t):
        return rcopy(ha_ref.at[prow(oy, t), col(c)], ha_ref.at[prow(oy, t), col(2 + c)],
                     x2_ss.at[t], x2_rs.at[t], dev_x)

    def d2_copy(t, pos):
        return rcopy(ha_ref.at[prow(oy, t), col(c)], ha_ref.at[prow(oy, t), col(pos)],
                     d2_ss.at[t], d2_rs.at[t], dev_d)

    def f2_copy(t, pos):
        return rcopy(ha_ref.at[prow(oy, t), col(2 + c)], ha_ref.at[prow(oy, t), col(2 + pos)],
                     f2_ss.at[t], f2_rs.at[t], dev_d)

    def got_y(t):
        y_wait(t)
        x2_copy(t).start()
        d2_copy(t, c).start()

    def got_x(t):
        x2_copy(t).wait_recv()
        f2_copy(t, c).start()

    def start_loop(n, f):
        lax.fori_loop(0, n, lambda i, s: (f(i), s)[1], 0)

    own_w = pltpu.make_async_copy(w_ref.at[pl.ds(pl.multiple_of(y * vocab, 16), vocab)], wv.at[:, whalf(y)], own_sem)
    draft_copy = rcopy(d_ref, dv, d_sem.at[0], d_sem.at[1], dev_y)
    draft_copy.start()
    start_loop(n_wc, lambda j: w_copy(j).start())
    start_loop(n_rb, lambda i: x1_copy(i).start())
    d1_copy(c).start()
    own_w.start()

    def pass_on(i):
        x1_copy(i).wait_recv()
        f1_copy(i, c).start()

    start_loop(n_rb, pass_on)
    d1_copy(oc).wait_recv()
    start_loop(n_rb, lambda i: f1_copy(i, oc).wait_recv())

    def load1(i, s):
        r = pl.ds(pl.multiple_of(i * R1, R1), R1)
        return (
            pltpu.make_async_copy(h_ref.at[r], hb.at[s, :, col(c)], ld_sem.at[s, 0]),
            pltpu.make_async_copy(ha_ref.at[rrow(i), col(oc)], hb.at[s, :, col(oc)], ld_sem.at[s, 1]),
            pltpu.make_async_copy(ha_ref.at[rrow(i), pl.ds(half, half)], hb.at[s, :, pl.ds(half, half)], ld_sem.at[s, 2]),
        )

    def load2(b, s):
        r = pl.ds(pl.multiple_of(oy * rows + b * R2, R2), R2)
        return pltpu.make_async_copy(ha_ref.at[r], hb.at[s, pl.ds(0, R2)], ld_sem.at[s, 0])

    def score(t, v0, hblk, want, st):
        mx, sm, pk = st
        n = want.shape[1]
        wt = wv[pl.ds(pl.multiple_of(v0, 16), t), :]
        lg = lax.dot_general(wt, hblk, (((1,), (1,)), ((), ())), preferred_element_type=jnp.float32)
        lg = lg.reshape(t // 8, 8, n)
        new = jnp.maximum(mx, jnp.max(lg, axis=0))
        sm = sm * jnp.exp(mx - new) + jnp.sum(jnp.exp(lg - new[None]), axis=0)
        ids = lax.broadcasted_iota(jnp.int32, (t // 8, 8, n), 0) * 8 + lax.broadcasted_iota(jnp.int32, (t // 8, 8, n), 1)
        pk = pk + jnp.sum(jnp.where(ids == (want - v0)[None], lg, 0.0), axis=0)
        return new, sm, pk

    def fresh(n):
        return jnp.full((8, n), -jnp.inf, jnp.float32), jnp.zeros((8, n), jnp.float32), jnp.zeros((8, n), jnp.float32)

    def squeeze(st):
        mx, sm, pk = st
        top = jnp.max(mx, axis=0, keepdims=True)
        return top, jnp.sum(sm * jnp.exp(mx - top), axis=0, keepdims=True), jnp.sum(pk, axis=0, keepdims=True)

    def step1(t, v0, i, s):
        @pl.when(v0 == 0)
        def _():
            for k, a in enumerate(fresh(R1)):
                st1[i, k] = a

        want = jnp.broadcast_to(d_ref[:, pl.ds(pl.multiple_of(i * R1, R1), R1)] - base, (8, R1))
        st = score(t, v0, hb[s], want, (st1[i, 0], st1[i, 1], st1[i, 2]))
        for k in range(3):
            st1[i, k] = st[k]

    def fetch1(i, s, last):
        nxt = lax.rem(i + 1, n_rb)

        @pl.when(jnp.logical_not(last))
        def _():
            for cp in load1(nxt, 1 - s):
                cp.start()

        for cp in load1(i, s):
            cp.wait()

    n_pair = (n_wc - 2) // 2
    for cp in load1(0, 0):
        cp.start()
    own_w.wait()

    def pairs(n, carry):
        j, i, s = n // n_rb, lax.rem(n, n_rb), lax.rem(n, 2)

        @pl.when(n == n_pair * n_rb // 2)
        def _():
            start_loop(n_pc, lambda t: y_copy(t).start())

        @pl.when(i == 0)
        def _():
            w_wait(2 * j)
            w_wait(2 * j + 1)

        fetch1(i, s, False)
        step1(2 * WC, j * (2 * WC), i, s)
        return carry

    lax.fori_loop(0, n_pair * n_rb, pairs, 0)

    def singles(n, carry):
        j, i, s = 2 * n_pair + n // n_rb, lax.rem(n, n_rb), lax.rem(n, 2)

        @pl.when(i == 0)
        def _():
            w_wait(j)

        @pl.when(n == n_rb + 4)
        def _():
            got_y(0)

        @pl.when(n == n_rb + 7)
        def _():
            got_y(1)

        fetch1(i, s, n == 2 * n_rb - 1)
        step1(WC, j * WC, i, s)
        return carry

    lax.fori_loop(0, 2 * n_rb, singles, 0)

    slot = y * 4 + m

    def final1(i, carry):
        st = squeeze((st1[i, 0], st1[i, 1], st1[i, 2]))
        for u in range(R1 // R2):
            for k in range(3):
                sta[slot, i * (R1 // R2) + u, k:k + 1, :] = st[k][:, u * R2:(u + 1) * R2]
        return carry

    lax.fori_loop(0, n_rb, final1, 0)

    draft_copy.wait_recv()
    got_x(0)
    got_y(2)
    got_x(1)

    def sa_copy(k, sl):
        return rcopy(sta.at[sl], sta.at[sl], sa_ss.at[k - 1], sa_rs.at[k - 1], (y, peer(k)))

    for k in range(1, 4):
        sa_copy(k, slot).start()

    def arrived(b):
        for u in range(R2 // PIECE):
            t = b * (R2 // PIECE) + u
            d2_copy(t, oc).wait_recv()
            f2_copy(t, oc).wait_recv()

    arrived(0)
    load2(0, 0).start()

    def sb_copy(g, k, b0, nb, sl):
        part = pl.ds(b0, nb)
        return rcopy(stb.at[part], sta.at[sl, part], sb_ss.at[g, k], sb_rs.at[g, k], (oy, peer(k)))

    n_t2 = vocab // (2 * WC)

    def block2(b, carry):
        s = lax.rem(b, 2)
        load2(b, s).wait()

        @pl.when(b == n_b2 - 1)
        def _():
            for k in range(4):
                sb_copy(0, k, 0, n_b2 - 1, slot).start()

        want = jnp.broadcast_to(dv[:, pl.ds(pl.multiple_of(b * R2, R2), R2)] - base, (8, R2))

        def tile(j, st):
            @pl.when(jnp.logical_and(j == 0, 2 * b + 3 < n_pc))
            def _():
                got_y(2 * b + 3)

            @pl.when(jnp.logical_and(j == 1, 2 * b + 2 < n_pc))
            def _():
                got_x(2 * b + 2)

            @pl.when(jnp.logical_and(j == 2, 2 * b + 4 < n_pc))
            def _():
                got_y(2 * b + 4)

            @pl.when(jnp.logical_and(j == 3, 2 * b + 3 < n_pc))
            def _():
                got_x(2 * b + 3)

            @pl.when(jnp.logical_and(j == 4, b + 1 < n_b2))
            def _():
                arrived(b + 1)
                load2(b + 1, 1 - s).start()

            return score(2 * WC, j * (2 * WC), hb[s, pl.ds(0, R2), :], want, st)

        st = squeeze(lax.fori_loop(0, n_t2, tile, fresh(R2)))
        for k in range(3):
            stb[b, k:k + 1, :] = st[k]
        return carry

    lax.fori_loop(0, n_b2, block2, 0)
    for k in range(4):
        sb_copy(1, k, n_b2 - 1, 1, slot).start()

    for k in range(1, 4):
        sa_copy(k, y * 4 + peer(k)).wait_recv()
    for k in range(4):
        sb_copy(0, k, 0, n_b2 - 1, oy * 4 + peer(k)).wait_recv()
        sb_copy(1, k, n_b2 - 1, 1, oy * 4 + peer(k)).wait_recv()

    def combine(b, carry):
        tops = [sta[i, b, 0:1, :] for i in range(8)]
        top = functools.reduce(jnp.maximum, tops)
        tot = functools.reduce(jnp.add, [sta[i, b, 1:2, :] * jnp.exp(tops[i] - top) for i in range(8)])
        pick = functools.reduce(jnp.add, [sta[i, b, 2:3, :] for i in range(8)])
        at = pl.ds(pl.multiple_of(b * R2, R2), R2)
        lp = pick - (top + jnp.log(tot))
        lp_ref[:, at] = lp
        ac_ref[:, at] = jnp.minimum(1.0, jnp.exp(lp) / q_ref[:, at])
        return carry

    lax.fori_loop(0, n_b2, combine, 0)

    draft_copy.wait_send()
    start_loop(n_wc, lambda j: w_copy(j).wait_send())
    start_loop(n_rb, lambda i: x1_copy(i).wait_send())
    d1_copy(c).wait_send()
    start_loop(n_rb, lambda i: f1_copy(i, c).wait_send())

    def drain(t):
        y_copy(t).wait_send()
        x2_copy(t).wait_send()
        d2_copy(t, c).wait_send()
        f2_copy(t, c).wait_send()

    start_loop(n_pc, drain)
    for k in range(1, 4):
        sa_copy(k, slot).wait_send()
    for k in range(4):
        sb_copy(0, k, 0, n_b2 - 1, slot).wait_send()
        sb_copy(1, k, n_b2 - 1, 1, slot).wait_send()


def solution(mesh):
    def per_device(h_part, w_part, draft_loc, q_loc):
        rows, quarter = h_part.shape
        shard, half = w_part.shape
        n_wc, n_rb, n_pc, n_b2 = shard // 2 // WC, rows // R1, rows // PIECE, rows // R2
        dma = pltpu.SemaphoreType.DMA
        vmem = pl.BlockSpec(memory_space=pltpu.VMEM)
        hbm = pl.BlockSpec(memory_space=pl.ANY)
        lp, ac, _ = pl.pallas_call(
            functools.partial(_kernel, rows, quarter, shard, half),
            out_shape=(
                jax.ShapeDtypeStruct((1, rows), jnp.float32),
                jax.ShapeDtypeStruct((1, rows), jnp.float32),
                jax.ShapeDtypeStruct((2 * rows, 2 * half), jnp.bfloat16),
            ),
            in_specs=[hbm, hbm, vmem, vmem],
            out_specs=(vmem, vmem, hbm),
            scratch_shapes=[
                pltpu.VMEM((shard // 2, 2 * half), jnp.bfloat16),
                pltpu.VMEM((2, R1, 2 * half), jnp.bfloat16),
                pltpu.VMEM((1, rows), jnp.int32),
                pltpu.VMEM((n_rb, 3, 8, R1), jnp.float32),
                pltpu.VMEM((8, n_b2, 8, R2), jnp.float32),
                pltpu.VMEM((n_b2, 8, R2), jnp.float32),
                dma, dma((2, 3)), dma((2,)), dma((n_wc,)), dma((n_wc,)), dma((n_pc,)), dma((n_pc,)),
                dma((n_rb,)), dma((n_rb,)), dma, dma, dma((n_rb,)), dma((n_rb,)),
                dma((n_pc,)), dma((n_pc,)), dma((n_pc,)), dma((n_pc,)), dma((n_pc,)), dma((n_pc,)),
                dma((3,)), dma((3,)), dma((2, 4)), dma((2, 4)),
            ],
            compiler_params=pltpu.CompilerParams(collective_id=0, has_side_effects=True, vmem_limit_bytes=67043328),
        )(h_part, w_part, draft_loc.reshape(1, rows), q_loc.reshape(1, rows))
        return lp.reshape(rows), ac.reshape(rows)

    return jax.shard_map(per_device, mesh=mesh, in_specs=(P("data", "model"), P("model", "data"), P("data"), P("data")), out_specs=(P("data"), P("data")), check_vma=False)
```

time: 1620 us -> 726 us (0.45)
  waiting for transfers between devices: 1180 us -> 0 us
  Pallas kernels: 0 us -> 722 us
  matrix products: 356 us -> 0 us
  other arithmetic: 41.7 us -> 0 us
  blocking collectives: 21 us -> 0 us
    all_gather x2 -> x0, waiting for transfers between devices: 1180 us -> none  [the longest x1 932 us: per_device(): w_rows = lax.all_gather(w_part, 'data', axis=1, tiled=True)]
    pallas_call x0 -> x1, Pallas kernels: none -> 722 us  [per_device(): pl.pallas_call(functools.partial(_kernel, rows, quarter, shard, half), ou...]
    dot_general x1 -> x0, matrix products: 356 us -> none  [per_device(): lax.dot_general(h_rows, w_rows, (((1,), (1,)), ((), ())), preferred_eleme...]
    reduce_sum x1 -> x0, other arithmetic: 40.5 us -> none  [per_device(): local_sum = jnp.sum(jnp.exp(logits - row_max[:, None]), axis=1)]
  transfers between devices with their start and end apart: 2 -> 0, of which waited for: 2 -> 0; matrix products, arithmetic and copies ran while one was open for 0% -> 0% of each run, Pallas kernels for 0% -> 0%
where the time goes in v1:
time: 726 us
  Pallas kernels  722 us (99%)
    pallas_call x1, Pallas kernels, per_device(): pl.pallas_call(functools.partial(_kernel, rows, quarter, shard, half), ou...  722 us

profile of v1, /device:TPU:0, one launch (start us, length us, event | category | flops | bytes accessed | tf_op | source)
XLA Modules:
  0.0 725.7 jit_solution(15011814574032707797)
XLA Ops:
  0.6 722.4 %shard_map.59 = (f32[1,4096]{1,0:T(1,128)}, f32[1,4096]{1,0:T(1,128)}, bf16[8192,5120]{1,0:T(8,128)(2,1)}) custom-call(bf16[4096,1280]{1,0:T(8,128)(2,1)} %h_ref.1, bf16[8000,2560]{1,0:T(8,128)(2,1)} %w_ref.1, s32[1,4096]{1,0:T(1,128)} %bitcast.4, f32[1,4096]{1,0:T(1,128)} %bitcast.5), custom_call_target="tpu_custom_call" | custom-call | tf_op jit(solution)/shard_map/pallas_call | solution.py:358
  723.1 1.3 copy.8
  724.4 1.3 copy.9

commit v2 on v1

--- a/solution.py
+++ b/solution.py
@@ -10,11 +10,12 @@
 MESH = pl.DeviceIdType.MESH
 WC = 400
 R1 = 512
-PIECE = 128
+PIECE = 64
 R2 = 256
-
-
-def _kernel(rows, quarter, shard, half, h_ref, w_ref, d_ref, q_ref, lp_ref, ac_ref, ha_ref,
+LANES = 128
+
+
+def _kernel(rows, quarter, shard, half, h_ref, w_ref, d_ref, pick_ref, lse_ref, ha_ref,
             wv, hb, dv, st1, sta, stb, own_sem, ld_sem, d_sem, w_ss, w_rs, y_ss, y_rs,
             x1_ss, x1_rs, d1_ss, d1_rs, f1_ss, f1_rs, x2_ss, x2_rs, d2_ss, d2_rs, f2_ss, f2_rs,
             sa_ss, sa_rs, sb_ss, sb_rs):
@@ -101,14 +102,24 @@
         return rcopy(ha_ref.at[prow(oy, t), col(2 + c)], ha_ref.at[prow(oy, t), col(2 + pos)],
                      f2_ss.at[t], f2_rs.at[t], dev_d)
 
-    def got_y(t):
-        y_wait(t)
-        x2_copy(t).start()
-        d2_copy(t, c).start()
-
-    def got_x(t):
-        x2_copy(t).wait_recv()
-        f2_copy(t, c).start()
+    def got_y(t, when=True):
+        @pl.when(when)
+        def _():
+            y_wait(t)
+            x2_copy(t).start()
+            d2_copy(t, c).start()
+
+    def got_x(t, when=True):
+        @pl.when(when)
+        def _():
+            x2_copy(t).wait_recv()
+            f2_copy(t, c).start()
+
+    def drain(t):
+        y_copy(t).wait_send()
+        x2_copy(t).wait_send()
+        d2_copy(t, c).wait_send()
+        f2_copy(t, c).wait_send()
 
     def start_loop(n, f):
         lax.fori_loop(0, n, lambda i, s: (f(i), s)[1], 0)
@@ -213,35 +224,38 @@
         def _():
             w_wait(j)
 
-        @pl.when(n == n_rb + 4)
-        def _():
-            got_y(0)
-
-        @pl.when(n == n_rb + 7)
-        def _():
-            got_y(1)
+        for at, ys, xs in ((1, (0,), ()), (3, (1,), ()), (4, (2,), (0,)), (6, (3,), (1,)), (7, (4,), (2,))):
+            @pl.when(n == n_rb + at)
+            def _():
+                for t in ys:
+                    got_y(t)
+                for t in xs:
+                    got_x(t)
 
         fetch1(i, s, n == 2 * n_rb - 1)
         step1(WC, j * WC, i, s)
         return carry
 
     lax.fori_loop(0, 2 * n_rb, singles, 0)
+    got_y(5)
+    got_x(3)
 
     slot = y * 4 + m
 
     def final1(i, carry):
         st = squeeze((st1[i, 0], st1[i, 1], st1[i, 2]))
-        for u in range(R1 // R2):
+        for u in range(R1 // LANES):
             for k in range(3):
-                sta[slot, i * (R1 // R2) + u, k:k + 1, :] = st[k][:, u * R2:(u + 1) * R2]
+                sta[slot, k, pl.ds(i * (R1 // LANES) + u, 1), :] = st[k][:, u * LANES:(u + 1) * LANES]
         return carry
 
     lax.fori_loop(0, n_rb, final1, 0)
 
     draft_copy.wait_recv()
-    got_x(0)
-    got_y(2)
-    got_x(1)
+    start_loop(n_wc, lambda j: w_copy(j).wait_send())
+    start_loop(n_rb, lambda i: x1_copy(i).wait_send())
+    d1_copy(c).wait_send()
+    start_loop(n_rb, lambda i: f1_copy(i, c).wait_send())
 
     def sa_copy(k, sl):
         return rcopy(sta.at[sl], sta.at[sl], sa_ss.at[k - 1], sa_rs.at[k - 1], (y, peer(k)))
@@ -258,41 +272,41 @@
     arrived(0)
     load2(0, 0).start()
 
-    def sb_copy(g, k, b0, nb, sl):
-        part = pl.ds(b0, nb)
-        return rcopy(stb.at[part], sta.at[sl, part], sb_ss.at[g, k], sb_rs.at[g, k], (oy, peer(k)))
+    parts = (pl.ds(0, rows // LANES - 8), pl.ds(rows // LANES - 8, 8))
+
+    def sb_copy(g, k, sl):
+        return rcopy(stb.at[:, parts[g]], sta.at[sl, :, parts[g]], sb_ss.at[g, k], sb_rs.at[g, k], (oy, peer(k)))
 
     n_t2 = vocab // (2 * WC)
 
     def block2(b, carry):
         s = lax.rem(b, 2)
+        got_x(4 * b + 4, 4 * b + 4 < n_pc)
+        got_y(4 * b + 6, 4 * b + 6 < n_pc)
         load2(b, s).wait()
 
-        @pl.when(b == n_b2 - 1)
+        @pl.when(b == n_b2 - 2)
         def _():
             for k in range(4):
-                sb_copy(0, k, 0, n_b2 - 1, slot).start()
+                sb_copy(0, k, slot).start()
+
+        @pl.when(b >= 4)
+        def _():
+            for u in range(R2 // PIECE):
+                drain((b - 4) * (R2 // PIECE) + u)
 
         want = jnp.broadcast_to(dv[:, pl.ds(pl.multiple_of(b * R2, R2), R2)] - base, (8, R2))
 
         def tile(j, st):
-            @pl.when(jnp.logical_and(j == 0, 2 * b + 3 < n_pc))
-            def _():
-                got_y(2 * b + 3)
-
-            @pl.when(jnp.logical_and(j == 1, 2 * b + 2 < n_pc))
-            def _():
-                got_x(2 * b + 2)
-
-            @pl.when(jnp.logical_and(j == 2, 2 * b + 4 < n_pc))
-            def _():
-                got_y(2 * b + 4)
-
-            @pl.when(jnp.logical_and(j == 3, 2 * b + 3 < n_pc))
-            def _():
-                got_x(2 * b + 3)
-
-            @pl.when(jnp.logical_and(j == 4, b + 1 < n_b2))
+            more = b + 1 < n_b2
+            got_x(4 * b + 5, jnp.logical_and(j == 1, more))
+            got_y(4 * b + 7, jnp.logical_and(j == 1, more))
+            got_x(4 * b + 6, jnp.logical_and(j == 2, more))
+            got_y(4 * b + 8, jnp.logical_and(j == 2, 4 * b + 8 < n_pc))
+            got_x(4 * b + 7, jnp.logical_and(j == 3, more))
+            got_y(4 * b + 9, jnp.logical_and(j == 3, 4 * b + 9 < n_pc))
+
+            @pl.when(jnp.logical_and(j == 4, more))
             def _():
                 arrived(b + 1)
                 load2(b + 1, 1 - s).start()
@@ -300,84 +314,68 @@
             return score(2 * WC, j * (2 * WC), hb[s, pl.ds(0, R2), :], want, st)
 
         st = squeeze(lax.fori_loop(0, n_t2, tile, fresh(R2)))
-        for k in range(3):
-            stb[b, k:k + 1, :] = st[k]
+        for u in range(R2 // LANES):
+            for k in range(3):
+                stb[k, pl.ds(b * (R2 // LANES) + u, 1), :] = st[k][:, u * LANES:(u + 1) * LANES]
         return carry
 
     lax.fori_loop(0, n_b2, block2, 0)
-    for k in range(4):
-        sb_copy(1, k, n_b2 - 1, 1, slot).start()
-
+
+    draft_copy.wait_send()
+    for u in range(4 * (R2 // PIECE)):
+        drain((n_b2 - 4) * (R2 // PIECE) + u)
     for k in range(1, 4):
+        sa_copy(k, slot).wait_send()
         sa_copy(k, y * 4 + peer(k)).wait_recv()
     for k in range(4):
-        sb_copy(0, k, 0, n_b2 - 1, oy * 4 + peer(k)).wait_recv()
-        sb_copy(1, k, n_b2 - 1, 1, oy * 4 + peer(k)).wait_recv()
-
-    def combine(b, carry):
-        tops = [sta[i, b, 0:1, :] for i in range(8)]
-        top = functools.reduce(jnp.maximum, tops)
-        tot = functools.reduce(jnp.add, [sta[i, b, 1:2, :] * jnp.exp(tops[i] - top) for i in range(8)])
-        pick = functools.reduce(jnp.add, [sta[i, b, 2:3, :] for i in range(8)])
-        at = pl.ds(pl.multiple_of(b * R2, R2), R2)
-        lp = pick - (top + jnp.log(tot))
-        lp_ref[:, at] = lp
-        ac_ref[:, at] = jnp.minimum(1.0, jnp.exp(lp) / q_ref[:, at])
-        return carry
-
-    lax.fori_loop(0, n_b2, combine, 0)
-
-    draft_copy.wait_send()
-    start_loop(n_wc, lambda j: w_copy(j).wait_send())
-    start_loop(n_rb, lambda i: x1_copy(i).wait_send())
-    d1_copy(c).wait_send()
-    start_loop(n_rb, lambda i: f1_copy(i, c).wait_send())
-
-    def drain(t):
-        y_copy(t).wait_send()
-        x2_copy(t).wait_send()
-        d2_copy(t, c).wait_send()
-        f2_copy(t, c).wait_send()
-
-    start_loop(n_pc, drain)
-    for k in range(1, 4):
-        sa_copy(k, slot).wait_send()
+        sb_copy(0, k, slot).wait_send()
+        sb_copy(0, k, oy * 4 + peer(k)).wait_recv()
     for k in range(4):
-        sb_copy(0, k, 0, n_b2 - 1, slot).wait_send()
-        sb_copy(1, k, n_b2 - 1, 1, slot).wait_send()
+        sb_copy(1, k, slot).start()
+    for k in range(4):
+        sb_copy(1, k, oy * 4 + peer(k)).wait_recv()
+
+    tops = [sta[i, 0] for i in range(8)]
+    top = functools.reduce(jnp.maximum, tops)
+    tot = functools.reduce(jnp.add, [sta[i, 1] * jnp.exp(tops[i] - top) for i in range(8)])
+    lse_ref[...] = top + jnp.log(tot)
+    pick_ref[...] = functools.reduce(jnp.add, [sta[i, 2] for i in range(8)])
+    for k in range(4):
+        sb_copy(1, k, slot).wait_send()
 
 
 def solution(mesh):
     def per_device(h_part, w_part, draft_loc, q_loc):
         rows, quarter = h_part.shape
         shard, half = w_part.shape
-        n_wc, n_rb, n_pc, n_b2 = shard // 2 // WC, rows // R1, rows // PIECE, rows // R2
+        n_wc, n_rb, n_pc = shard // 2 // WC, rows // R1, rows // PIECE
         dma = pltpu.SemaphoreType.DMA
         vmem = pl.BlockSpec(memory_space=pltpu.VMEM)
         hbm = pl.BlockSpec(memory_space=pl.ANY)
-        lp, ac, _ = pl.pallas_call(
+        pick, lse, _ = pl.pallas_call(
             functools.partial(_kernel, rows, quarter, shard, half),
             out_shape=(
-                jax.ShapeDtypeStruct((1, rows), jnp.float32),
-                jax.ShapeDtypeStruct((1, rows), jnp.float32),
+                jax.ShapeDtypeStruct((rows // LANES, LANES), jnp.float32),
+                jax.ShapeDtypeStruct((rows // LANES, LANES), jnp.float32),
                 jax.ShapeDtypeStruct((2 * rows, 2 * half), jnp.bfloat16),
             ),
-            in_specs=[hbm, hbm, vmem, vmem],
+            in_specs=[hbm, hbm, vmem],
             out_specs=(vmem, vmem, hbm),
             scratch_shapes=[
                 pltpu.VMEM((shard // 2, 2 * half), jnp.bfloat16),
                 pltpu.VMEM((2, R1, 2 * half), jnp.bfloat16),
                 pltpu.VMEM((1, rows), jnp.int32),
                 pltpu.VMEM((n_rb, 3, 8, R1), jnp.float32),
-                pltpu.VMEM((8, n_b2, 8, R2), jnp.float32),
-                pltpu.VMEM((n_b2, 8, R2), jnp.float32),
+                pltpu.VMEM((8, 3, rows // LANES, LANES), jnp.float32),
+                pltpu.VMEM((3, rows // LANES, LANES), jnp.float32),
                 dma, dma((2, 3)), dma((2,)), dma((n_wc,)), dma((n_wc,)), dma((n_pc,)), dma((n_pc,)),
                 dma((n_rb,)), dma((n_rb,)), dma, dma, dma((n_rb,)), dma((n_rb,)),
                 dma((n_pc,)), dma((n_pc,)), dma((n_pc,)), dma((n_pc,)), dma((n_pc,)), dma((n_pc,)),
                 dma((3,)), dma((3,)), dma((2, 4)), dma((2, 4)),
             ],
             compiler_params=pltpu.CompilerParams(collective_id=0, has_side_effects=True, vmem_limit_bytes=67043328),
-        )(h_part, w_part, draft_loc.reshape(1, rows), q_loc.reshape(1, rows))
-        return lp.reshape(rows), ac.reshape(rows)
+        )(h_part, w_part, draft_loc.reshape(1, rows))
+        log_prob = pick.reshape(rows) - lse.reshape(rows)
+        return log_prob, jnp.minimum(1.0, jnp.exp(log_prob) / q_loc)
 
     return jax.shard_map(per_device, mesh=mesh, in_specs=(P("data", "model"), P("model", "data"), P("data"), P("data")), out_specs=(P("data"), P("data")), check_vma=False)

time: 726 us -> 712 us (0.981)
  Pallas kernels: 722 us -> 710 us
    pallas_call x1, Pallas kernels: 722 us -> 710 us  [per_device(): pl.pallas_call(functools.partial(_kernel, rows, quarter, shard, half), ou...]
where the time goes in v2:
time: 712 us
  Pallas kernels  710 us (100%)
    pallas_call x1, Pallas kernels, per_device(): pl.pallas_call(functools.partial(_kernel, rows, quarter, shard, half), ou...  710 us

profile of v2, /device:TPU:0, one launch (start us, length us, event | category | flops | bytes accessed | tf_op | source)
XLA Modules:
  0.0 711.7 jit_solution(3116757414554944059)
XLA Ops:
  0.6 709.6 %shard_map.59 = (f32[32,128]{1,0:T(8,128)}, f32[32,128]{1,0:T(8,128)}, bf16[8192,5120]{1,0:T(8,128)(2,1)}) custom-call(bf16[4096,1280]{1,0:T(8,128)(2,1)} %h_ref.1, bf16[8000,2560]{1,0:T(8,128)(2,1)} %w_ref.1, s32[1,4096]{1,0:T(1,128)} %bitcast.4), custom_call_target="tpu_custom_call" | custom-call | tf_op jit(solution)/shard_map/pallas_call | solution.py:355
  710.3 1.4 divide_minimum_fusion

commit v3 on v0

v3 whole, which is shorter than its diff:
```python
import functools

import jax
import jax.numpy as jnp
from jax import lax
from jax.experimental import pallas as pl
from jax.experimental.pallas import tpu as pltpu
from jax.sharding import PartitionSpec as P

MESH = pl.DeviceIdType.MESH
WT = 752
WL = 240
RX = 512
PIECE = 64
R = 256
LANES = 128
PIECE_T, HOP_T, STEP1_T, STEP2_T, START2_T, SLACK_T = 350, 900, 250, 256, 4500, 30


def _kernel(rows, quarter, shard, half, h_ref, w_ref, d_ref, pick_ref, lse_ref, ha_ref,
            wv, hb, part, dv, st, sta, stb, own_sem, ld_sem, d_sem, w_ss, w_rs, y_ss, y_rs,
            x1_ss, x1_rs, d1_ss, d1_rs, f1_ss, f1_rs, x2_ss, x2_rs, d2_ss, d2_rs, f2_ss, f2_rs,
            sa_ss, sa_rs, sb_ss, sb_rs):
    y = lax.axis_index("data")
    m = lax.axis_index("model")
    x = m // 2
    c = m % 2
    oy = 1 - y
    dev_y = (oy, m)
    dev_x = (y, (1 - x) * 2 + c)
    dev_d = (y, x * 2 + 1 - c)
    vocab = shard // 2
    base = m * shard + y * vocab
    n_wt = (vocab - WL) // WT
    vl = n_wt * WT
    n_x1 = rows // RX
    n_pc = rows // PIECE
    n_b = rows // R

    def col(p):
        return pl.ds(pl.multiple_of(p * quarter, 128), quarter)

    xy = lax.rem(x + y, 2)
    mine = xy * 2 + c
    core = xy * 2 + 1 - c
    far = (1 - xy) * 2 + c
    farcore = (1 - xy) * 2 + 1 - c
    own_cols, other_cols = pl.ds(0, half), pl.ds(half, half)

    def peer(k):
        kx, kc = k // 2, k % 2
        return lax.rem(x + kx, 2) * 2 + lax.rem(c + kc, 2)

    bar = pltpu.get_barrier_semaphore()
    for dy in range(2):
        for k in range(4):
            if dy or k:
                pl.semaphore_signal(bar, 1, device_id=(lax.rem(y + dy, 2), peer(k)), device_id_type=MESH)
    pl.semaphore_wait(bar, 7)

    def rcopy(src, dst, ss, rs, dev):
        return pltpu.make_async_remote_copy(src, dst, ss, rs, device_id=dev, device_id_type=MESH)

    def rds(start, n, to=16):
        return pl.ds(pl.multiple_of(start, to), n)

    def w_copy(j):
        return rcopy(w_ref.at[rds(oy * vocab + j * WT, WT)], wv.at[rds(j * WT, WT), other_cols],
                     w_ss.at[j], w_rs.at[j], dev_y)

    wl_copy = rcopy(w_ref.at[rds(oy * vocab + vl, WL)], wv.at[pl.ds(vl, WL), other_cols],
                    w_ss.at[n_wt], w_rs.at[n_wt], dev_y)

    def prow(yy, t):
        return rds(yy * rows + t * PIECE, PIECE, PIECE)

    def y_copy(t):
        return rcopy(h_ref.at[rds(t * PIECE, PIECE, PIECE)], ha_ref.at[prow(y, t), col(far)],
                     y_ss.at[t], y_rs.at[t], dev_y)

    def y_wait(t):
        rcopy(h_ref.at[pl.ds(0, PIECE)], ha_ref.at[prow(oy, t), col(mine)], y_ss.at[t], y_rs.at[t], dev_y).wait_recv()

    def rrow(i):
        return rds(y * rows + i * RX, RX, RX)

    def x1_copy(i, pos):
        return rcopy(h_ref.at[rds(i * RX, RX, RX)], ha_ref.at[rrow(i), col(pos)], x1_ss.at[i], x1_rs.at[i], dev_x)

    def d1_copy(pos):
        return rcopy(h_ref, ha_ref.at[rds(y * rows, rows, RX), col(pos)], d1_ss, d1_rs, dev_d)

    def f1_copy(i, pos):
        return rcopy(ha_ref.at[rrow(i), col(far)], ha_ref.at[rrow(i), col(pos)], f1_ss.at[i], f1_rs.at[i], dev_d)

    def x2_copy(t, pos):
        return rcopy(ha_ref.at[prow(oy, t), col(mine)], ha_ref.at[prow(oy, t), col(pos)],
                     x2_ss.at[t], x2_rs.at[t], dev_x)

    def d2_copy(t, pos):
        return rcopy(ha_ref.at[prow(oy, t), col(mine)], ha_ref.at[prow(oy, t), col(pos)],
                     d2_ss.at[t], d2_rs.at[t], dev_d)

    def f2_copy(t, pos):
        return rcopy(ha_ref.at[prow(oy, t), col(far)], ha_ref.at[prow(oy, t), col(pos)],
                     f2_ss.at[t], f2_rs.at[t], dev_d)

    def got_y(t):
        y_wait(t)
        x2_copy(t, mine).start()
        d2_copy(t, mine).start()

    def got_x(t):
        x2_copy(t, far).wait_recv()
        f2_copy(t, far).start()

    def drain(t):
        y_copy(t).wait_send()
        x2_copy(t, mine).wait_send()
        d2_copy(t, mine).wait_send()
        f2_copy(t, far).wait_send()

    def span(lo, hi, f):
        lax.fori_loop(lo, hi, lambda i, s: (f(i), s)[1], 0)

    def due(now, least):
        ny = jnp.minimum(n_pc, jnp.maximum((now + SLACK_T) // PIECE_T, least))
        nx = jnp.minimum(n_pc, jnp.maximum(jnp.maximum(now - HOP_T, 0) // PIECE_T, least))
        return ny, nx

    def pass_pieces(before, after):
        span(before[0], after[0], got_y)
        span(before[1], after[1], got_x)

    own_w = pltpu.make_async_copy(w_ref.at[rds(y * vocab, vocab)], wv.at[:, own_cols], own_sem)
    draft_copy = rcopy(d_ref, dv, d_sem.at[0], d_sem.at[1], dev_y)
    draft_copy.start()
    span(0, n_wt, lambda j: w_copy(j).start())
    span(0, n_x1, lambda i: x1_copy(i, mine).start())
    d1_copy(mine).start()
    own_w.start()

    def own_in(i):
        s = lax.rem(i, 4)
        return pltpu.make_async_copy(h_ref.at[rds(i * R, R, R)], hb.at[s, :, pl.ds(0, quarter)], ld_sem.at[s, 0])

    def own_out(i):
        s = lax.rem(i, 4)
        return pltpu.make_async_copy(hb.at[s, :, pl.ds(0, quarter)], ha_ref.at[rds(y * rows + i * R, R, R), col(mine)], ld_sem.at[s, 1])

    def own_step(i):
        @pl.when(i >= 4)
        def _():
            own_out(i - 4).wait()

        @pl.when(i < n_b)
        def _():
            own_in(i).start()
            own_in(i).wait()
            own_out(i).start()

    span(0, n_b + 4, own_step)

    def pass_on(i):
        x1_copy(i, far).wait_recv()
        f1_copy(i, far).start()

    span(0, n_x1, pass_on)
    d1_copy(core).wait_recv()
    span(0, n_x1, lambda i: f1_copy(i, farcore).wait_recv())
    own_w.wait()

    def load(yy, i, s):
        return pltpu.make_async_copy(ha_ref.at[rds(yy * rows + i * R, R, R)], hb.at[s], ld_sem.at[s, 0])

    def dot(a, b):
        return lax.dot_general(a, b, (((1,), (1,)), ((), ())), preferred_element_type=jnp.float32)

    def update(lg, v0, want, old):
        mx, sm, pk = old
        t = lg.shape[0]
        lg = lg.reshape(t // 8, 8, R)
        new = jnp.maximum(mx, jnp.max(lg, axis=0))
        sm = sm * jnp.exp(mx - new) + jnp.sum(jnp.exp(lg - new[None]), axis=0)
        ids = lax.broadcasted_iota(jnp.int32, (t // 8, 8, R), 0) * 8 + lax.broadcasted_iota(jnp.int32, (t // 8, 8, R), 1)
        pk = pk + jnp.sum(jnp.where(ids == (want - v0)[None], lg, 0.0), axis=0)
        return new, sm, pk

    def fresh():
        return jnp.full((8, R), -jnp.inf, jnp.float32), jnp.zeros((8, R), jnp.float32), jnp.zeros((8, R), jnp.float32)

    def first_part(b, s):
        part[b] = dot(wv[pl.ds(vl, WL), own_cols], hb[s, :, own_cols])

    load(y, 0, 0).start()

    def step1(n, carry):
        j, i, s = n // n_b, lax.rem(n, n_b), lax.rem(n, 2)

        @pl.when(n == n_b)
        def _():
            span(0, n_pc, lambda t: y_copy(t).start())
            wl_copy.start()

        @pl.when(i == 0)
        def _():
            w_copy(j).wait_recv()

        @pl.when(jnp.logical_and(j == n_wt - 1, i > 0))
        def _():
            pass_pieces(due((i - 1) * STEP1_T, 0), due(i * STEP1_T, 0))

        @pl.when(n + 1 < n_wt * n_b)
        def _():
            load(y, lax.rem(i + 1, n_b), 1 - s).start()

        load(y, i, s).wait()

        @pl.when(j == 0)
        def _():
            for k, a in enumerate(fresh()):
                st[i, k] = a
            first_part(i, s)

        want = jnp.broadcast_to(d_ref[:, rds(i * R, R, R)] - base, (8, R))
        new = update(dot(wv[rds(j * WT, WT), :], hb[s]), j * WT, want, (st[i, 0], st[i, 1], st[i, 2]))
        for k in range(3):
            st[i, k] = new[k]
        return carry

    lax.fori_loop(0, n_wt * n_b, step1, 0)

    draft_copy.wait_recv()
    span(0, n_wt, lambda j: w_copy(j).wait_send())
    span(0, n_x1, lambda i: x1_copy(i, mine).wait_send())
    d1_copy(mine).wait_send()
    span(0, n_x1, lambda i: f1_copy(i, far).wait_send())

    per = R // PIECE

    def arrived(b):
        for u in range(per):
            d2_copy(b * per + u, core).wait_recv()
            f2_copy(b * per + u, farcore).wait_recv()

    arrived(0)
    load(oy, 0, 0).start()

    def block2(b, carry):
        s = lax.rem(b, 2)
        load(oy, b, s).wait()
        first_part(n_b + b, s)
        want = jnp.broadcast_to(dv[:, rds(b * R, R, R)] - base, (8, R))

        @pl.when(b >= 4)
        def _():
            for u in range(per):
                drain((b - 4) * per + u)

        def tile(j, old):
            now = START2_T + (b * n_wt + j) * STEP2_T
            least = (b + 1) * per
            before = jnp.where(b + j == 0, (n_b - 1) * STEP1_T, now - STEP2_T)
            pass_pieces(due(before, least), due(now, least + per * (j // (n_wt - 1))))

            @pl.when(jnp.logical_and(j == n_wt - 1, b + 1 < n_b))
            def _():
                arrived(b + 1)
                load(oy, b + 1, 1 - s).start()

            return update(dot(wv[rds(j * WT, WT), :], hb[s]), j * WT, want, old)

        new = lax.fori_loop(0, n_wt, tile, fresh())
        for k in range(3):
            st[n_b + b, k] = new[k]
        return carry

    lax.fori_loop(0, n_b, block2, 0)

    n_g = n_b // 2

    def load_pair(g):
        s = lax.rem(g, 4)
        r = lax.rem(oy + g // n_g, 2) * rows + lax.rem(g, n_g) * (2 * R)
        return [pltpu.make_async_copy(ha_ref.at[rds(r + u * R, R, R), other_cols], hb.at[s, :, pl.ds(u * half, half)],
                                      ld_sem.at[s, u]) for u in range(2)]

    for g in range(3):
        for cp in load_pair(g):
            cp.start()
    for u in range(4 * per):
        drain((n_b - 4) * per + u)
    draft_copy.wait_send()

    slot = y * 4 + m
    n_row = rows // LANES
    parts = (pl.ds(0, n_row - 8), pl.ds(n_row - 8, 8))

    def sb_copy(k, sl):
        return rcopy(stb, sta.at[sl], sb_ss.at[k], sb_rs.at[k], (oy, peer(k)))

    def sa_copy(g, k, sl):
        return rcopy(sta.at[sl, :, parts[g]], sta.at[sl, :, parts[g]], sa_ss.at[g, k - 1], sa_rs.at[g, k - 1], (y, peer(k)))

    def last(g, first, ids_ref, out):
        s = lax.rem(g, 4)

        @pl.when(g + 3 < 2 * n_g)
        def _():
            for cp in load_pair(g + 3):
                cp.start()

        for cp in load_pair(g):
            cp.wait()
        w = wv[pl.ds(vl, WL), other_cols]
        for u in range(2):
            i = lax.rem(g, n_g) * 2 + u
            b = first + i
            want = jnp.broadcast_to(ids_ref[:, rds(i * R, R, R)] - base, (8, R))
            lg = part[b] + dot(w, hb[s, :, u * half:(u + 1) * half])
            mx, sm, pk = update(lg, vl, want, (st[b, 0], st[b, 1], st[b, 2]))
            top = jnp.max(mx, axis=0, keepdims=True)
            res = (top, jnp.sum(sm * jnp.exp(mx - top), axis=0, keepdims=True), jnp.sum(pk, axis=0, keepdims=True))
            for v in range(R // LANES):
                for k in range(3):
                    out[k, pl.ds(i * (R // LANES) + v, 1), :] = res[k][:, v * LANES:(v + 1) * LANES]

    wl_copy.wait_recv()
    span(0, n_g, lambda g: last(g, n_b, dv, stb))

    def last_own(g):
        @pl.when(g == n_g + 1)
        def _():
            for k in range(4):
                sb_copy(k, slot).start()

        @pl.when(g == 2 * n_g - 1)
        def _():
            for k in range(1, 4):
                sa_copy(0, k, slot).start()

        last(g, 0, d_ref, sta.at[slot])

    span(n_g, 2 * n_g, last_own)

    wl_copy.wait_send()
    for k in range(4):
        sb_copy(k, slot).wait_send()
        sb_copy(k, oy * 4 + peer(k)).wait_recv()
    for k in range(1, 4):
        sa_copy(1, k, slot).start()
    for g in range(2):
        for k in range(1, 4):
            sa_copy(g, k, y * 4 + peer(k)).wait_recv()

    tops = [sta[i, 0] for i in range(8)]
    top = functools.reduce(jnp.maximum, tops)
    tot = functools.reduce(jnp.add, [sta[i, 1] * jnp.exp(tops[i] - top) for i in range(8)])
    lse_ref[...] = top + jnp.log(tot)
    pick_ref[...] = functools.reduce(jnp.add, [sta[i, 2] for i in range(8)])
    for g in range(2):
        for k in range(1, 4):
            sa_copy(g, k, slot).wait_send()


def solution(mesh):
    def per_device(h_part, w_part, draft_loc, q_loc):
        rows, quarter = h_part.shape
        shard, half = w_part.shape
        n_w, n_x1, n_pc, n_b = (shard // 2 - WL) // WT + 1, rows // RX, rows // PIECE, rows // R
        dma = pltpu.SemaphoreType.DMA
        vmem = pl.BlockSpec(memory_space=pltpu.VMEM)
        hbm = pl.BlockSpec(memory_space=pl.ANY)
        sums = jax.ShapeDtypeStruct((rows // LANES, LANES), jnp.float32)
        pick, lse, _ = pl.pallas_call(
            functools.partial(_kernel, rows, quarter, shard, half),
            out_shape=(sums, sums, jax.ShapeDtypeStruct((2 * rows, 2 * half), jnp.bfloat16)),
            in_specs=[hbm, hbm, vmem],
            out_specs=(vmem, vmem, hbm),
            scratch_shapes=[
                pltpu.VMEM((shard // 2, 2 * half), jnp.bfloat16),
                pltpu.VMEM((4, R, 2 * half), jnp.bfloat16),
                pltpu.VMEM((2 * n_b, WL, R), jnp.float32),
                pltpu.VMEM((1, rows), jnp.int32),
                pltpu.VMEM((2 * n_b, 3, 8, R), jnp.float32),
                pltpu.VMEM((8, 3, rows // LANES, LANES), jnp.float32),
                pltpu.VMEM((3, rows // LANES, LANES), jnp.float32),
                dma, dma((4, 2)), dma((2,)), dma((n_w,)), dma((n_w,)), dma((n_pc,)), dma((n_pc,)),
                dma((n_x1,)), dma((n_x1,)), dma, dma, dma((n_x1,)), dma((n_x1,)),
                dma((n_pc,)), dma((n_pc,)), dma((n_pc,)), dma((n_pc,)), dma((n_pc,)), dma((n_pc,)),
                dma((2, 3)), dma((2, 3)), dma((4,)), dma((4,)),
            ],
            compiler_params=pltpu.CompilerParams(collective_id=0, has_side_effects=True, vmem_limit_bytes=67043328),
        )(h_part, w_part, draft_loc.reshape(1, rows))
        log_prob = pick.reshape(rows) - lse.reshape(rows)
        return log_prob, jnp.minimum(1.0, jnp.exp(log_prob) / q_loc)

    return jax.shard_map(per_device, mesh=mesh, in_specs=(P("data", "model"), P("model", "data"), P("data"), P("data")), out_specs=(P("data"), P("data")), check_vma=False)
```

time: 1620 us -> 701 us (0.43)
  waiting for transfers between devices: 1180 us -> 0 us
  Pallas kernels: 0 us -> 698 us
  matrix products: 356 us -> 0 us
  other arithmetic: 41.7 us -> 1.37 us
  blocking collectives: 21 us -> 0 us
    all_gather x2 -> x0, waiting for transfers between devices: 1180 us -> none  [the longest x1 932 us: per_device(): w_rows = lax.all_gather(w_part, 'data', axis=1, tiled=True)]
    pallas_call x0 -> x1, Pallas kernels: none -> 698 us  [per_device(): pl.pallas_call(functools.partial(_kernel, rows, quarter, shard, half), ou...]
    dot_general x1 -> x0, matrix products: 356 us -> none  [per_device(): lax.dot_general(h_rows, w_rows, (((1,), (1,)), ((), ())), preferred_eleme...]
    reduce_sum x1 -> x0, other arithmetic: 40.5 us -> none  [per_device(): local_sum = jnp.sum(jnp.exp(logits - row_max[:, None]), axis=1)]
  transfers between devices with their start and end apart: 2 -> 0, of which waited for: 2 -> 0; matrix products, arithmetic and copies ran while one was open for 0% -> 0% of each run, Pallas kernels for 0% -> 0%
where the time goes in v3:
time: 701 us; the launch traced here: 700 us
  Pallas kernels  698 us (100%)
    pallas_call x1, Pallas kernels, per_device(): pl.pallas_call(functools.partial(_kernel, rows, quarter, shard, half), ou...  698 us

profile of v3, /device:TPU:0, one launch (start us, length us, event | category | flops | bytes accessed | tf_op | source)
XLA Modules:
  0.0 700.0 jit_solution(9176606371483465077)
XLA Ops:
  0.6 698.0 %shard_map.59 = (f32[32,128]{1,0:T(8,128)}, f32[32,128]{1,0:T(8,128)}, bf16[8192,5120]{1,0:T(8,128)(2,1)}) custom-call(bf16[4096,1280]{1,0:T(8,128)(2,1)} %h_ref.1, bf16[8000,2560]{1,0:T(8,128)(2,1)} %w_ref.1, s32[1,4096]{1,0:T(1,128)} %bitcast.4), custom_call_target="tpu_custom_call" | custom-call | tf_op jit(solution)/shard_map/pallas_call | solution.py:375
  698.6 1.4 divide_minimum_fusion

commit v4 on v3

--- a/solution.py
+++ b/solution.py
@@ -17,8 +17,8 @@
 PIECE_T, HOP_T, STEP1_T, STEP2_T, START2_T, SLACK_T = 350, 900, 250, 256, 4500, 30
 
 
-def _kernel(rows, quarter, shard, half, h_ref, w_ref, d_ref, pick_ref, lse_ref, ha_ref,
-            wv, hb, part, dv, st, sta, stb, own_sem, ld_sem, d_sem, w_ss, w_rs, y_ss, y_rs,
+def _kernel(rows, quarter, shard, half, h_ref, w_ref, dh_ref, pick_ref, lse_ref, ha_ref,
+            wv, hb, part, d_ref, dv, st, sta, stb, own_sem, ld_sem, d_sem, w_ss, w_rs, y_ss, y_rs,
             x1_ss, x1_rs, d1_ss, d1_rs, f1_ss, f1_rs, x2_ss, x2_rs, d2_ss, d2_rs, f2_ss, f2_rs,
             sa_ss, sa_rs, sb_ss, sb_rs):
     y = lax.axis_index("data")
@@ -133,8 +133,10 @@
         span(before[1], after[1], got_x)
 
     own_w = pltpu.make_async_copy(w_ref.at[rds(y * vocab, vocab)], wv.at[:, own_cols], own_sem)
-    draft_copy = rcopy(d_ref, dv, d_sem.at[0], d_sem.at[1], dev_y)
+    draft_copy = rcopy(dh_ref, dv, d_sem.at[0], d_sem.at[1], dev_y)
+    own_d = pltpu.make_async_copy(dh_ref, d_ref, d_sem.at[2])
     draft_copy.start()
+    own_d.start()
     span(0, n_wt, lambda j: w_copy(j).start())
     span(0, n_x1, lambda i: x1_copy(i, mine).start())
     d1_copy(mine).start()
@@ -169,6 +171,7 @@
     d1_copy(core).wait_recv()
     span(0, n_x1, lambda i: f1_copy(i, farcore).wait_recv())
     own_w.wait()
+    own_d.wait()
 
     def load(yy, i, s):
         return pltpu.make_async_copy(ha_ref.at[rds(yy * rows + i * R, R, R)], hb.at[s], ld_sem.at[s, 0])
@@ -293,16 +296,24 @@
     draft_copy.wait_send()
 
     slot = y * 4 + m
-    n_row = rows // LANES
-    parts = (pl.ds(0, n_row - 8), pl.ds(n_row - 8, 8))
+    n_eight = n_b // 8
 
     def sb_copy(k, sl):
         return rcopy(stb, sta.at[sl], sb_ss.at[k], sb_rs.at[k], (oy, peer(k)))
 
     def sa_copy(g, k, sl):
-        return rcopy(sta.at[sl, :, parts[g]], sta.at[sl, :, parts[g]], sa_ss.at[g, k - 1], sa_rs.at[g, k - 1], (y, peer(k)))
-
-    def last(g, first, ids_ref, out):
+        eight = sta.at[sl, :, :, pl.ds(g * 8, 8)]
+        return rcopy(eight, eight, sa_ss.at[g, k - 1], sa_rs.at[g, k - 1], (y, peer(k)))
+
+    def squeeze(b, out, g):
+        mx, sm, pk = (st[pl.ds(b, 8), k] for k in range(3))
+        top = jnp.max(mx, axis=1)
+        res = (top, jnp.sum(sm * jnp.exp(mx - top[:, None]), axis=1), jnp.sum(pk, axis=1))
+        for k in range(3):
+            for v in range(R // LANES):
+                out[k, v, pl.ds(g * 8, 8), :] = res[k][:, v * LANES:(v + 1) * LANES]
+
+    def last(g, first, ids_ref):
         s = lax.rem(g, 4)
 
         @pl.when(g + 3 < 2 * n_g)
@@ -313,20 +324,19 @@
         for cp in load_pair(g):
             cp.wait()
         w = wv[pl.ds(vl, WL), other_cols]
+        i = lax.rem(g, n_g) * 2
+        lgs = [part[first + i + u] + dot(w, hb[s, :, u * half:(u + 1) * half]) for u in range(2)]
+        olds = [tuple(st[first + i + u, k] for k in range(3)) for u in range(2)]
+        wants = [jnp.broadcast_to(ids_ref[:, rds((i + u) * R, R, R)] - base, (8, R)) for u in range(2)]
+        news = [update(lgs[u], vl, wants[u], olds[u]) for u in range(2)]
         for u in range(2):
-            i = lax.rem(g, n_g) * 2 + u
-            b = first + i
-            want = jnp.broadcast_to(ids_ref[:, rds(i * R, R, R)] - base, (8, R))
-            lg = part[b] + dot(w, hb[s, :, u * half:(u + 1) * half])
-            mx, sm, pk = update(lg, vl, want, (st[b, 0], st[b, 1], st[b, 2]))
-            top = jnp.max(mx, axis=0, keepdims=True)
-            res = (top, jnp.sum(sm * jnp.exp(mx - top), axis=0, keepdims=True), jnp.sum(pk, axis=0, keepdims=True))
-            for v in range(R // LANES):
-                for k in range(3):
-                    out[k, pl.ds(i * (R // LANES) + v, 1), :] = res[k][:, v * LANES:(v + 1) * LANES]
+            for k in range(3):
+                st[first + i + u, k] = news[u][k]
 
     wl_copy.wait_recv()
-    span(0, n_g, lambda g: last(g, n_b, dv, stb))
+    span(0, n_g, lambda g: last(g, n_b, dv))
+    for g in range(n_eight):
+        squeeze(n_b + g * 8, stb, g)
 
     def last_own(g):
         @pl.when(g == n_g + 1)
@@ -334,31 +344,43 @@
             for k in range(4):
                 sb_copy(k, slot).start()
 
-        @pl.when(g == 2 * n_g - 1)
-        def _():
-            for k in range(1, 4):
-                sa_copy(0, k, slot).start()
-
-        last(g, 0, d_ref, sta.at[slot])
+        @pl.when(g == 2 * n_g - 4)
+        def _():
+            for h in range(n_eight - 1):
+                squeeze(h * 8, sta.at[slot], h)
+
+        @pl.when(g == 2 * n_g - 2)
+        def _():
+            for h in range(n_eight - 1):
+                for k in range(1, 4):
+                    sa_copy(h, k, slot).start()
+
+        last(g, 0, d_ref)
 
     span(n_g, 2 * n_g, last_own)
+    squeeze((n_eight - 1) * 8, sta.at[slot], n_eight - 1)
 
     wl_copy.wait_send()
     for k in range(4):
         sb_copy(k, slot).wait_send()
         sb_copy(k, oy * 4 + peer(k)).wait_recv()
     for k in range(1, 4):
-        sa_copy(1, k, slot).start()
-    for g in range(2):
+        sa_copy(n_eight - 1, k, slot).start()
+    for g in range(n_eight):
         for k in range(1, 4):
             sa_copy(g, k, y * 4 + peer(k)).wait_recv()
 
     tops = [sta[i, 0] for i in range(8)]
     top = functools.reduce(jnp.maximum, tops)
     tot = functools.reduce(jnp.add, [sta[i, 1] * jnp.exp(tops[i] - top) for i in range(8)])
-    lse_ref[...] = top + jnp.log(tot)
-    pick_ref[...] = functools.reduce(jnp.add, [sta[i, 2] for i in range(8)])
-    for g in range(2):
+    lse = top + jnp.log(tot)
+    pick = functools.reduce(jnp.add, [sta[i, 2] for i in range(8)])
+    for i in range(n_b):
+        for v in range(R // LANES):
+            r = i * (R // LANES) + v
+            lse_ref[r:r + 1, :] = lse[v, i:i + 1, :]
+            pick_ref[r:r + 1, :] = pick[v, i:i + 1, :]
+    for g in range(n_eight):
         for k in range(1, 4):
             sa_copy(g, k, slot).wait_send()
 
@@ -375,20 +397,21 @@
         pick, lse, _ = pl.pallas_call(
             functools.partial(_kernel, rows, quarter, shard, half),
             out_shape=(sums, sums, jax.ShapeDtypeStruct((2 * rows, 2 * half), jnp.bfloat16)),
-            in_specs=[hbm, hbm, vmem],
+            in_specs=[hbm, hbm, hbm],
             out_specs=(vmem, vmem, hbm),
             scratch_shapes=[
                 pltpu.VMEM((shard // 2, 2 * half), jnp.bfloat16),
                 pltpu.VMEM((4, R, 2 * half), jnp.bfloat16),
                 pltpu.VMEM((2 * n_b, WL, R), jnp.float32),
                 pltpu.VMEM((1, rows), jnp.int32),
+                pltpu.VMEM((1, rows), jnp.int32),
                 pltpu.VMEM((2 * n_b, 3, 8, R), jnp.float32),
-                pltpu.VMEM((8, 3, rows // LANES, LANES), jnp.float32),
-                pltpu.VMEM((3, rows // LANES, LANES), jnp.float32),
-                dma, dma((4, 2)), dma((2,)), dma((n_w,)), dma((n_w,)), dma((n_pc,)), dma((n_pc,)),
+                pltpu.VMEM((8, 3, R // LANES, n_b, LANES), jnp.float32),
+                pltpu.VMEM((3, R // LANES, n_b, LANES), jnp.float32),
+                dma, dma((4, 2)), dma((3,)), dma((n_w,)), dma((n_w,)), dma((n_pc,)), dma((n_pc,)),
                 dma((n_x1,)), dma((n_x1,)), dma, dma, dma((n_x1,)), dma((n_x1,)),
                 dma((n_pc,)), dma((n_pc,)), dma((n_pc,)), dma((n_pc,)), dma((n_pc,)), dma((n_pc,)),
-                dma((2, 3)), dma((2, 3)), dma((4,)), dma((4,)),
+                dma((n_b // 8, 3)), dma((n_b // 8, 3)), dma((4,)), dma((4,)),
             ],
             compiler_params=pltpu.CompilerParams(collective_id=0, has_side_effects=True, vmem_limit_bytes=67043328),
         )(h_part, w_part, draft_loc.reshape(1, rows))

time: 701 us -> 700 us (level)
  no operation moved by 1% of the time
where the time goes in v4:
time: 700 us; the launch traced here: 699 us
  Pallas kernels  697 us (100%)
    pallas_call x1, Pallas kernels, per_device(): pl.pallas_call(functools.partial(_kernel, rows, quarter, shard, half), ou...  697 us

profile of v4, /device:TPU:0, one launch (start us, length us, event | category | flops | bytes accessed | tf_op | source)
XLA Modules:
  0.0 699.4 jit_solution(17859992045336441101)
XLA Ops:
  0.6 697.4 %shard_map.59 = (f32[32,128]{1,0:T(8,128)}, f32[32,128]{1,0:T(8,128)}, bf16[8192,5120]{1,0:T(8,128)(2,1)}) custom-call(bf16[4096,1280]{1,0:T(8,128)(2,1)} %h_ref.1, bf16[8000,2560]{1,0:T(8,128)(2,1)} %w_ref.1, s32[1,4096]{1,0:T(1,128)} %bitcast.4), custom_call_target="tpu_custom_call" | custom-call | tf_op jit(solution)/shard_map/pallas_call | solution.py:397
  698.1 1.4 divide_minimum_fusion
